TPU v7x, 32 devices: a whole 2x2x4 slice. The times are simulated.
32 devices in a mesh: grp: 2 (over x), mem: 16 (over z, y, core).
Axes of the slice: x: 2, y: 2, z: 4, core: 2. Of those that a mesh axis runs over, the one named last changes fastest.
Arguments:
- phi_owned: float32 [8, 8, 8, 4096], P(None, None, None, ('grp', 'mem')), may hold values from -6 to 6
- band_counts: int32 [2, 16], P('grp'), may hold values from 1 to 128, 512 in all within a row
- neighbours: int32 [2, 6, 512], P('grp'), may hold values from -1 to 1023, as said below
Outputs:
- phi_new: float32 [8, 8, 8, 4096], P(None, None, None, ('grp', 'mem'))
Inputs may be any that keep to these rules, and one draw needn't show every extreme that they name: `band_counts`: in every group the counts sum to 512, each is at least 1, and the largest is exactly 128. `neighbours`: tile k of a group lies at column k mod 16 and row k // 16 of the group's tile sheet. An entry is -1 (no neighbour) or the id of the tile across that face: tile k - 1, k + 1, k - 16, k + 16 of the same group for faces 0 to 3 (never across an edge of the sheet), tile k of group g - 1 or g + 1 for faces 4 and 5. Links are mutual.
All inputs are finite; a program needn't handle non-finite values.
Results may differ from a plain program's by a relative error of at most 0.0003.
Values sent between devices are 32-bit elements; how exact they have to be, the bound alone decides.
A program may use at most 64 MiB of HBM per device.

v0:
```python
import jax
import jax.numpy as jnp
from jax import lax
from jax.sharding import PartitionSpec as P

STEPS = 4


TIME_STEP = 0.5
EPSILON = 1e-06


def with_halo(x, sides, width):
    for axis, dim in sides:
        devices, length = (lax.axis_size(axis), x.shape[dim])
        up = [(i, (i + 1) % devices) for i in range(devices - 1)]
        down = [(j, i) for i, j in up]
        last = lax.slice_in_dim(x, length - width, length, axis=dim)
        leading = lax.slice_in_dim(x, 0, width, axis=dim)
        before = lax.ppermute(last, axis, up)
        after = lax.ppermute(leading, axis, down)
        x = jnp.concatenate([before, x, after], axis=dim)
    return x


def upwind(backward, forward, positive):
    rising = jnp.maximum(
        jnp.square(jnp.maximum(backward, 0.0)), jnp.square(jnp.minimum(forward, 0.0))
    )
    falling = jnp.maximum(
        jnp.square(jnp.minimum(backward, 0.0)), jnp.square(jnp.maximum(forward, 0.0))
    )
    return jnp.where(positive, rising, falling)


def advance(level_set, sign_field, ghosts, present, slots):
    tile_edge = level_set.shape[0]
    positive = sign_field > 0
    wide_mask = [jnp.tile(present[face_index], tile_edge) for face_index in range(4)]
    below_x = jnp.where(wide_mask[0], ghosts[0], level_set[0])
    above_x = jnp.where(wide_mask[1], ghosts[1], level_set[tile_edge - 1])
    extended = jnp.concatenate([below_x[None], level_set, above_x[None]], axis=0)
    squares = upwind(level_set - extended[:tile_edge], extended[2:] - level_set, positive)
    below_y = jnp.where(wide_mask[2], ghosts[2], level_set[:, 0])
    above_y = jnp.where(wide_mask[3], ghosts[3], level_set[:, tile_edge - 1])
    extended = jnp.concatenate([below_y[:, None], level_set, above_y[:, None]], axis=1)
    squares = squares + upwind(
        level_set - extended[:, :tile_edge], extended[:, 2:] - level_set, positive
    )
    below_z = jnp.where(present[4], ghosts[4], level_set[:, :, :slots])
    above_z = jnp.where(present[5], ghosts[5], level_set[:, :, -slots:])
    backward = level_set - jnp.concatenate([below_z, level_set[:, :, :-slots]], axis=2)
    forward = jnp.concatenate([level_set[:, :, slots:], above_z], axis=2) - level_set
    squares = squares + upwind(backward, forward, positive)
    return level_set - TIME_STEP * sign_field * (jnp.sqrt(squares + EPSILON) - 1.0)


def outgoing(payload, first_tile, columns):
    leading = payload.shape[:-1]
    blocks = payload.reshape(leading + (payload.shape[-1] // columns, columns))
    return jnp.roll(blocks, first_tile % columns, axis=-1)


def incoming(returned, first_tile, columns):
    leading = returned.shape[:-2]
    blocks = jnp.roll(returned, -(first_tile % columns), axis=-1)
    return blocks.reshape(leading + (returned.shape[-2] * columns,))


def arrival(starts, column_index, columns, row_count):
    tile_ids = jnp.arange(row_count, dtype=jnp.int32) * columns + column_index
    owner_mask = (starts[None, :] <= tile_ids[:, None]).astype(jnp.int32)
    owner_of = jnp.sum(owner_mask, axis=1) - 1
    picked = (jnp.arange(columns, dtype=jnp.int32)[None, :] == owner_of[:, None]).astype(jnp.int32)
    first_tile = jnp.sum(picked * starts[None, :], axis=1)
    return (tile_ids - first_tile) // columns * columns + owner_of


def departure(starts, counts, column_index, columns, depth):
    offset = (column_index - starts[None, :]) % columns + jnp.arange(depth, dtype=jnp.int32)[
        :, None
    ] * columns
    sheet_row = (starts[None, :] + offset) // columns
    return jnp.where(offset < counts[None, :], sheet_row, 0).reshape(-1)


def on_device(phi_owned, band_counts, neighbours):
    tile_edge = phi_owned.shape[0]
    own_slots = phi_owned.shape[3]
    columns = lax.axis_size("mem")
    column_index = lax.axis_index("mem")
    depth = own_slots // columns
    tile_total = neighbours.shape[2]
    row_count = tile_total // columns
    counts = band_counts[0]
    starts = jnp.cumsum(counts) - counts
    first_tile = lax.dynamic_index_in_dim(starts, column_index, 0, keepdims=False)
    my_count = lax.dynamic_index_in_dim(counts, column_index, 0, keepdims=False)
    arrive = arrival(starts, column_index, columns, row_count)
    depart = departure(starts, counts, column_index, columns, depth)
    link_table = neighbours[0]
    held_links = (
        lax.dynamic_index_in_dim(
            link_table.reshape(6, row_count, columns), column_index, 2, keepdims=False
        )
        >= 0
    )
    received = lax.all_to_all(
        outgoing(phi_owned, first_tile, columns), "mem", split_axis=4, concat_axis=4, tiled=True
    )
    holder_tiles = jnp.take(
        received.reshape(tile_edge, tile_edge, tile_edge, own_slots), arrive, axis=3
    )
    level_set = holder_tiles.reshape(tile_edge, tile_edge, tile_edge * row_count)
    sign_field = level_set / jnp.sqrt(level_set * level_set + 1.0)
    for sweep in range(STEPS):
        padded_columns = with_halo(level_set, (("mem", 0),), 1)
        padded_groups = with_halo(level_set, (("grp", 2),), row_count)
        upper = level_set[:, tile_edge - 1].reshape(tile_edge, tile_edge, row_count)
        lower = level_set[:, 0].reshape(tile_edge, tile_edge, row_count)
        ghosts = (
            padded_columns[0],
            padded_columns[tile_edge + 1],
            jnp.roll(upper, 1, axis=2).reshape(tile_edge, -1),
            jnp.roll(lower, -1, axis=2).reshape(tile_edge, -1),
            padded_groups[:, :, :row_count],
            padded_groups[:, :, -row_count:],
        )
        level_set = advance(level_set, sign_field, ghosts, held_links, row_count)
    final_tiles = level_set.reshape(tile_edge, tile_edge, tile_edge, row_count)
    leaving = jnp.take(final_tiles, depart, axis=3).reshape(
        tile_edge, tile_edge, tile_edge, depth, columns
    )
    returned = lax.all_to_all(leaving, "mem", split_axis=4, concat_axis=4, tiled=True)
    result = incoming(returned, first_tile, columns)
    live = jnp.arange(own_slots, dtype=jnp.int32) < my_count
    return jnp.where(live, result, 0.0)


def solution(mesh):
    return jax.shard_map(
        on_device,
        mesh=mesh,
        in_specs=(P(None, None, None, ("grp", "mem")), P("grp", None), P("grp", None, None)),
        out_specs=P(None, None, None, ("grp", "mem")),
        check_vma=False,
    )
```

profile of v0, /device:TPU:0, one launch (start us, length us, event | category | flops | bytes accessed | tf_op | source)
XLA Modules:
  0.0 150.3 jit_solution(7183766868067175868)
XLA Ops:
  4.1 2.9 %reshape.412 = f32[8,8,8,8,16]{4,3,2,1,0:T(8,128)} reshape(f32[8,8,8,128]{3,2,1,0:T(8,128)} %param.5) | data formatting | bytes 524288 | tf_op jit(solution)/shard_map/reshape | solution.py:60
  7.0 3.4 %dynamic-slice_maximum_fusion.1 = f32[8,8,8,8,16]{4,3,2,1,0:T(8,128)S(1)} fusion(s32[]{:T(128)S(6)} %select_n.315, f32[8,8,8,8,16]{4,3,2,1,0:T(8,128)} %reshape.412), kind=kLoop, calls=%fused_computation.4 | loop fusion | flops 65536 | bytes 524292 | tf_op jit(solution)/shard_map/jit(_roll_dynamic)/concatenate | solution.py:61
  10.3 4.4 %copy.40 = f32[8,8,8,8,16]{2,1,3,0,4:T(8,128)} copy(f32[8,8,8,8,16]{4,3,2,1,0:T(8,128)S(1)} %dynamic-slice_maximum_fusion.1) | data formatting | bytes 524288
  14.8 4.4 %reshape.458 = f32[16,1,4096]{2,1,0:T(1,128)} reshape(f32[16,8,8,8,8]{4,3,2,1,0:T(8,128)} %bitcast.56) | data formatting | bytes 524288
  19.2 7.4 %all-to-all-start = ((f32[16,1,4096]{2,1,0:T(1,128)}), f32[16,1,4096]{2,1,0:T(1,128)S(1)}, u32[]{:S(2)}, u32[]{:S(2)}) async-start(f32[16,1,4096]{2,1,0:T(1,128)} %reshape.458), calls=%async_computation | async-start | bytes 524288 | tf_op jit(solution)/shard_map/all_to_all | solution.py:108
  28.3 8.4 %all-to-all-done = f32[16,1,4096]{2,1,0:T(1,128)S(1)} async-done(((f32[16,1,4096]{2,1,0:T(1,128)}), f32[16,1,4096]{2,1,0:T(1,128)S(1)}, u32[]{:S(2)}, u32[]{:S(2)}) %all-to-all-start) | async-done | bytes 262176 | tf_op jit(solution)/shard_map/all_to_all | solution.py:108
  38.3 3.6 %reshape.459 = f32[16,8,8,8,8]{4,3,2,1,0:T(8,128)} reshape(f32[16,4096]{1,0:T(8,128)S(1)} %reduce.31) | data formatting | bytes 524288
  41.9 4.7 %copy.32 = f32[8,8,8,8,16]{2,1,4,3,0:T(8,128)} copy(f32[8,8,8,8,16]{2,1,3,0,4:T(8,128)} %bitcast.57) | data formatting | bytes 524288 | tf_op jit(solution)/shard_map/all_to_all | solution.py:108
  46.7 2.9 %gather_fusion = f32[32,8,8,8]{3,2,1,0:T(8,128)S(1)} fusion(f32[8,8,8,128]{2,1,3,0:T(8,128)} %bitcast.61, s32[1024]{0:T(1024)S(1)} %pad_clamp_fusion.1), kind=kCustom, calls=%fused_computation | custom fusion | bytes 131200 | tf_op jit(solution)/shard_map/jit(_take)/gather | solution.py:111
  50.6 3.4 %collective-permute-start.2 = (f32[8,8,32]{2,1,0:T(8,128)S(1)}, f32[8,8,32]{2,1,0:T(8,128)S(1)}, u32[]{:S(2)}, u32[]{:S(2)}) collective-permute-start(f32[8,8,32]{2,1,0:T(8,128)S(1)} %get-tuple-element.62), channel_id=1, source_target_pairs={{0,16},{1,17},{2,18},{3,19},{4,20},{5,21},{6,22},{7,23},{8,24},{9,... | collective-permute-start | bytes 24584 | tf_op jit(solution)/shard_map/ppermute | solution.py:20
  57.6 3.0 %collective-permute-start = (f32[1,8,256]{2,1,0:T(8,128)S(1)}, f32[1,8,256]{2,1,0:T(8,128)S(1)}, u32[]{:S(2)}, u32[]{:S(2)}) collective-permute-start(f32[1,8,256]{2,1,0:T(8,128)S(1)} %slice.284), channel_id=1, source_target_pairs={{0,1},{1,2},{2,3},{3,4},{4,5},{5,6},{6,7},{7,8},{8,9},{9,10},{10,1... | collective-permute-start | bytes 24584 | tf_op jit(solution)/shard_map/ppermute | solution.py:20
  62.0 4.5 %collective-permute-start.6 = (f32[8,8,32]{2,1,0:T(8,128)S(1)}, f32[8,8,32]{2,1,0:T(8,128)S(1)}, u32[]{:S(2)}, u32[]{:S(2)}) collective-permute-start(f32[8,8,32]{2,1,0:T(8,128)S(1)} %get-tuple-element.54), channel_id=1, source_target_pairs={{0,16},{1,17},{2,18},{3,19},{4,20},{5,21},{6,22},{7,23},{8,24},{9,... | collective-permute-start | bytes 24584 | tf_op jit(solution)/shard_map/ppermute | solution.py:20
  72.4 3.4 %collective-permute-done.5 = f32[1,8,256]{2,1,0:T(8,128)S(1)} collective-permute-done((f32[1,8,256]{2,1,0:T(8,128)S(1)}, f32[1,8,256]{2,1,0:T(8,128)S(1)}, u32[]{:S(2)}, u32[]{:S(2)}) %collective-permute-start.5) | collective-permute-done | bytes 8224 | tf_op jit(solution)/shard_map/ppermute | solution.py:21
  76.2 4.5 %collective-permute-start.10 = (f32[8,8,32]{2,1,0:T(8,128)S(1)}, f32[8,8,32]{2,1,0:T(8,128)S(1)}, u32[]{:S(2)}, u32[]{:S(2)}) collective-permute-start(f32[8,8,32]{2,1,0:T(8,128)S(1)} %get-tuple-element.42), channel_id=1, source_target_pairs={{0,16},{1,17},{2,18},{3,19},{4,20},{5,21},{6,22},{7,23},{8,24},{9,... | collective-permute-start | bytes 24584 | tf_op jit(solution)/shard_map/ppermute | solution.py:20
  82.7 4.0 %collective-permute-start.8 = (f32[1,8,256]{2,1,0:T(8,128)S(1)}, f32[1,8,256]{2,1,0:T(8,128)S(1)}, u32[]{:S(2)}, u32[]{:S(2)}) collective-permute-start(f32[1,8,256]{2,1,0:T(8,128)S(1)} %get-tuple-element.36), channel_id=1, source_target_pairs={{0,1},{1,2},{2,3},{3,4},{4,5},{5,6},{6,7},{7,8},{8,9},{9,10},{10,1... | collective-permute-start | bytes 24584 | tf_op jit(solution)/shard_map/ppermute | solution.py:20
  90.2 4.5 %collective-permute-start.14 = (f32[8,8,32]{2,1,0:T(8,128)S(1)}, f32[8,8,32]{2,1,0:T(8,128)S(1)}, u32[]{:S(2)}, u32[]{:S(2)}) collective-permute-start(f32[8,8,32]{2,1,0:T(8,128)S(1)} %get-tuple-element.30), channel_id=1, source_target_pairs={{0,16},{1,17},{2,18},{3,19},{4,20},{5,21},{6,22},{7,23},{8,24},{9,... | collective-permute-start | bytes 24584 | tf_op jit(solution)/shard_map/ppermute | solution.py:20
  96.6 5.0 %collective-permute-start.12 = (f32[1,8,256]{2,1,0:T(8,128)S(1)}, f32[1,8,256]{2,1,0:T(8,128)S(1)}, u32[]{:S(2)}, u32[]{:S(2)}) collective-permute-start(f32[1,8,256]{2,1,0:T(8,128)S(1)} %get-tuple-element.24), channel_id=1, source_target_pairs={{0,1},{1,2},{2,3},{3,4},{4,5},{5,6},{6,7},{7,8},{8,9},{9,10},{10,1... | collective-permute-start | bytes 24584 | tf_op jit(solution)/shard_map/ppermute | solution.py:20
  105.4 3.0 %gather_fusion.1 = f32[128,8,8,8]{3,2,1,0:T(8,128)} fusion(f32[8,8,8,32]{2,1,3,0:T(8,128)S(1)} %copy.36, s32[1024]{0:T(1024)S(1)} %pad_clamp_fusion), kind=kCustom, calls=%fused_computation.1 | custom fusion | bytes 524800 | tf_op jit(solution)/shard_map/jit(_take)/gather | solution.py:131
  108.5 4.5 %fusion.42 = f32[16,8,8,8,8]{4,3,2,1,0:T(8,128)} fusion(f32[8,8,8,8,16]{2,1,0,4,3:T(8,128)} %bitcast.60, pred[8,16]{0,1:T(8,128)(4,1)S(1)} %copy.30), kind=kLoop, calls=%fused_computation.167 | loop fusion | flops 65536 | bytes 524416
  113.0 4.4 %reshape.460 = f32[16,1,4096]{2,1,0:T(1,128)} reshape(f32[16,8,8,8,8]{4,3,2,1,0:T(8,128)} %fusion.42) | data formatting | bytes 524288
  117.4 7.6 %all-to-all-start.1 = ((f32[16,1,4096]{2,1,0:T(1,128)}), f32[16,1,4096]{2,1,0:T(1,128)S(1)}, u32[]{:S(2)}, u32[]{:S(2)}) async-start(f32[16,1,4096]{2,1,0:T(1,128)} %reshape.460), calls=%async_computation.1 | async-start | bytes 524288 | tf_op jit(solution)/shard_map/all_to_all | solution.py:134
  126.4 8.6 %all-to-all-done.1 = f32[16,1,4096]{2,1,0:T(1,128)S(1)} async-done(((f32[16,1,4096]{2,1,0:T(1,128)}), f32[16,1,4096]{2,1,0:T(1,128)S(1)}, u32[]{:S(2)}, u32[]{:S(2)}) %all-to-all-start.1) | async-done | bytes 262176 | tf_op jit(solution)/shard_map/all_to_all | solution.py:134
  136.2 3.6 %reshape.461 = f32[16,8,8,8,8]{4,3,2,1,0:T(8,128)} reshape(f32[16,4096]{1,0:T(8,128)S(1)} %reduce.32) | data formatting | bytes 524288
  139.8 5.0 %copy.38 = f32[8,8,8,8,16]{4,3,2,1,0:T(8,128)S(1)} copy(f32[8,8,8,8,16]{2,1,0,3,4:T(8,128)} %bitcast.58) | data formatting | bytes 524288 | tf_op jit(solution)/shard_map/all_to_all | solution.py:134
  (146 shorter events, 36.4 us)
Async XLA Ops:
  14.7 11.9 %copy-start.1 = (s32[1,16]{1,0:T(1,128)S(1)}, s32[1,16]{1,0:T(1,128)}, u32[]{:S(2)}) copy-start(s32[1,16]{1,0:T(1,128)} %param.6) | copy-start | bytes 196
  14.8 12.2 %copy-start = (s32[1,6,512]{2,0,1:T(1,128)S(1)}, s32[1,6,512]{2,0,1:T(1,128)}, u32[]{:S(2)}) copy-start(s32[1,6,512]{2,0,1:T(1,128)} %param.7) | copy-start | bytes 36868
  19.2 17.4 %all-to-all-start = ((f32[16,1,4096]{2,1,0:T(1,128)}), f32[16,1,4096]{2,1,0:T(1,128)S(1)}, u32[]{:S(2)}, u32[]{:S(2)}) async-start(f32[16,1,4096]{2,1,0:T(1,128)} %reshape.458), calls=%async_computation | async-start | bytes 524288 | tf_op jit(solution)/shard_map/all_to_all | solution.py:108
  50.6 10.9 %collective-permute-start.2 = (f32[8,8,32]{2,1,0:T(8,128)S(1)}, f32[8,8,32]{2,1,0:T(8,128)S(1)}, u32[]{:S(2)}, u32[]{:S(2)}) collective-permute-start(f32[8,8,32]{2,1,0:T(8,128)S(1)} %get-tuple-element.62), channel_id=1, source_target_pairs={{0,16},{1,17},{2,18},{3,19},{4,20},{5,21},{6,22},{7,23},{8,24},{9,... | collective-permute-start | bytes 24584 | tf_op jit(solution)/shard_map/ppermute | solution.py:20
  54.0 7.5 %collective-permute-start.3 = (f32[8,8,32]{2,1,0:T(8,128)S(1)}, f32[8,8,32]{2,1,0:T(8,128)S(1)}, u32[]{:S(2)}, u32[]{:S(2)}) collective-permute-start(f32[8,8,32]{2,1,0:T(8,128)S(1)} %get-tuple-element.63), channel_id=1, source_target_pairs={{16,0},{17,1},{18,2},{19,3},{20,4},{21,5},{22,6},{23,7},{24,8},{25... | collective-permute-start | bytes 24584 | tf_op jit(solution)/shard_map/ppermute | solution.py:21
  56.2 4.5 %collective-permute-start.1 = (f32[1,8,256]{2,1,0:T(8,128)S(1)}, f32[1,8,256]{2,1,0:T(8,128)S(1)}, u32[]{:S(2)}, u32[]{:S(2)}) collective-permute-start(f32[1,8,256]{2,1,0:T(8,128)S(1)} %squeeze.17), channel_id=1, source_target_pairs={{1,0},{2,1},{3,2},{4,3},{5,4},{6,5},{7,6},{8,7},{9,8},{10,9},{11,1... | collective-permute-start | bytes 24584 | tf_op jit(solution)/shard_map/ppermute | solution.py:21
  57.6 3.8 %collective-permute-start = (f32[1,8,256]{2,1,0:T(8,128)S(1)}, f32[1,8,256]{2,1,0:T(8,128)S(1)}, u32[]{:S(2)}, u32[]{:S(2)}) collective-permute-start(f32[1,8,256]{2,1,0:T(8,128)S(1)} %slice.284), channel_id=1, source_target_pairs={{0,1},{1,2},{2,3},{3,4},{4,5},{5,6},{6,7},{7,8},{8,9},{9,10},{10,1... | collective-permute-start | bytes 24584 | tf_op jit(solution)/shard_map/ppermute | solution.py:20
  62.0 10.0 %collective-permute-start.6 = (f32[8,8,32]{2,1,0:T(8,128)S(1)}, f32[8,8,32]{2,1,0:T(8,128)S(1)}, u32[]{:S(2)}, u32[]{:S(2)}) collective-permute-start(f32[8,8,32]{2,1,0:T(8,128)S(1)} %get-tuple-element.54), channel_id=1, source_target_pairs={{0,16},{1,17},{2,18},{3,19},{4,20},{5,21},{6,22},{7,23},{8,24},{9,... | collective-permute-start | bytes 24584 | tf_op jit(solution)/shard_map/ppermute | solution.py:20
  66.5 5.8 %collective-permute-start.7 = (f32[8,8,32]{2,1,0:T(8,128)S(1)}, f32[8,8,32]{2,1,0:T(8,128)S(1)}, u32[]{:S(2)}, u32[]{:S(2)}) collective-permute-start(f32[8,8,32]{2,1,0:T(8,128)S(1)} %get-tuple-element.55), channel_id=1, source_target_pairs={{16,0},{17,1},{18,2},{19,3},{20,4},{21,5},{22,6},{23,7},{24,8},{25... | collective-permute-start | bytes 24584 | tf_op jit(solution)/shard_map/ppermute | solution.py:21
  68.5 3.9 %collective-permute-start.4 = (f32[1,8,256]{2,1,0:T(8,128)S(1)}, f32[1,8,256]{2,1,0:T(8,128)S(1)}, u32[]{:S(2)}, u32[]{:S(2)}) collective-permute-start(f32[1,8,256]{2,1,0:T(8,128)S(1)} %get-tuple-element.48), channel_id=1, source_target_pairs={{0,1},{1,2},{2,3},{3,4},{4,5},{5,6},{6,7},{7,8},{8,9},{9,10},{10,1... | collective-permute-start | bytes 24584 | tf_op jit(solution)/shard_map/ppermute | solution.py:20
  70.7 5.1 %collective-permute-start.5 = (f32[1,8,256]{2,1,0:T(8,128)S(1)}, f32[1,8,256]{2,1,0:T(8,128)S(1)}, u32[]{:S(2)}, u32[]{:S(2)}) collective-permute-start(f32[1,8,256]{2,1,0:T(8,128)S(1)} %get-tuple-element.49), channel_id=1, source_target_pairs={{1,0},{2,1},{3,2},{4,3},{5,4},{6,5},{7,6},{8,7},{9,8},{10,9},{11,1... | collective-permute-start | bytes 24584 | tf_op jit(solution)/shard_map/ppermute | solution.py:21
  76.2 11.9 %collective-permute-start.10 = (f32[8,8,32]{2,1,0:T(8,128)S(1)}, f32[8,8,32]{2,1,0:T(8,128)S(1)}, u32[]{:S(2)}, u32[]{:S(2)}) collective-permute-start(f32[8,8,32]{2,1,0:T(8,128)S(1)} %get-tuple-element.42), channel_id=1, source_target_pairs={{0,16},{1,17},{2,18},{3,19},{4,20},{5,21},{6,22},{7,23},{8,24},{9,... | collective-permute-start | bytes 24584 | tf_op jit(solution)/shard_map/ppermute | solution.py:20
  80.7 7.3 %collective-permute-start.11 = (f32[8,8,32]{2,1,0:T(8,128)S(1)}, f32[8,8,32]{2,1,0:T(8,128)S(1)}, u32[]{:S(2)}, u32[]{:S(2)}) collective-permute-start(f32[8,8,32]{2,1,0:T(8,128)S(1)} %get-tuple-element.43), channel_id=1, source_target_pairs={{16,0},{17,1},{18,2},{19,3},{20,4},{21,5},{22,6},{23,7},{24,8},{25... | collective-permute-start | bytes 24584 | tf_op jit(solution)/shard_map/ppermute | solution.py:21
  82.7 5.5 %collective-permute-start.8 = (f32[1,8,256]{2,1,0:T(8,128)S(1)}, f32[1,8,256]{2,1,0:T(8,128)S(1)}, u32[]{:S(2)}, u32[]{:S(2)}) collective-permute-start(f32[1,8,256]{2,1,0:T(8,128)S(1)} %get-tuple-element.36), channel_id=1, source_target_pairs={{0,1},{1,2},{2,3},{3,4},{4,5},{5,6},{6,7},{7,8},{8,9},{9,10},{10,1... | collective-permute-start | bytes 24584 | tf_op jit(solution)/shard_map/ppermute | solution.py:20
  86.7 3.1 %collective-permute-start.9 = (f32[1,8,256]{2,1,0:T(8,128)S(1)}, f32[1,8,256]{2,1,0:T(8,128)S(1)}, u32[]{:S(2)}, u32[]{:S(2)}) collective-permute-start(f32[1,8,256]{2,1,0:T(8,128)S(1)} %get-tuple-element.37), channel_id=1, source_target_pairs={{1,0},{2,1},{3,2},{4,3},{5,4},{6,5},{7,6},{8,7},{9,8},{10,9},{11,1... | collective-permute-start | bytes 24584 | tf_op jit(solution)/shard_map/ppermute | solution.py:21
  90.2 13.0 %collective-permute-start.14 = (f32[8,8,32]{2,1,0:T(8,128)S(1)}, f32[8,8,32]{2,1,0:T(8,128)S(1)}, u32[]{:S(2)}, u32[]{:S(2)}) collective-permute-start(f32[8,8,32]{2,1,0:T(8,128)S(1)} %get-tuple-element.30), channel_id=1, source_target_pairs={{0,16},{1,17},{2,18},{3,19},{4,20},{5,21},{6,22},{7,23},{8,24},{9,... | collective-permute-start | bytes 24584 | tf_op jit(solution)/shard_map/ppermute | solution.py:20
  94.7 8.5 %collective-permute-start.15 = (f32[8,8,32]{2,1,0:T(8,128)S(1)}, f32[8,8,32]{2,1,0:T(8,128)S(1)}, u32[]{:S(2)}, u32[]{:S(2)}) collective-permute-start(f32[8,8,32]{2,1,0:T(8,128)S(1)} %get-tuple-element.31), channel_id=1, source_target_pairs={{16,0},{17,1},{18,2},{19,3},{20,4},{21,5},{22,6},{23,7},{24,8},{25... | collective-permute-start | bytes 24584 | tf_op jit(solution)/shard_map/ppermute | solution.py:21
  96.6 6.7 %collective-permute-start.12 = (f32[1,8,256]{2,1,0:T(8,128)S(1)}, f32[1,8,256]{2,1,0:T(8,128)S(1)}, u32[]{:S(2)}, u32[]{:S(2)}) collective-permute-start(f32[1,8,256]{2,1,0:T(8,128)S(1)} %get-tuple-element.24), channel_id=1, source_target_pairs={{0,1},{1,2},{2,3},{3,4},{4,5},{5,6},{6,7},{7,8},{8,9},{9,10},{10,1... | collective-permute-start | bytes 24584 | tf_op jit(solution)/shard_map/ppermute | solution.py:20
  101.7 3.1 %collective-permute-start.13 = (f32[1,8,256]{2,1,0:T(8,128)S(1)}, f32[1,8,256]{2,1,0:T(8,128)S(1)}, u32[]{:S(2)}, u32[]{:S(2)}) collective-permute-start(f32[1,8,256]{2,1,0:T(8,128)S(1)} %get-tuple-element.25), channel_id=1, source_target_pairs={{1,0},{2,1},{3,2},{4,3},{5,4},{6,5},{7,6},{8,7},{9,8},{10,9},{11,1... | collective-permute-start | bytes 24584 | tf_op jit(solution)/shard_map/ppermute | solution.py:21
  117.4 17.6 %all-to-all-start.1 = ((f32[16,1,4096]{2,1,0:T(1,128)}), f32[16,1,4096]{2,1,0:T(1,128)S(1)}, u32[]{:S(2)}, u32[]{:S(2)}) async-start(f32[16,1,4096]{2,1,0:T(1,128)} %reshape.460), calls=%async_computation.1 | async-start | bytes 524288 | tf_op jit(solution)/shard_map/all_to_all | solution.py:134
where the time goes:
time: 151 us; the launch traced here: 150 us
  starting transfers between devices  56.7 us (38%)
  local copies, waits for them, and re-layouts  49 us (32%)
  waiting for transfers between devices  24.6 us (16%)
  other arithmetic  17.4 us (12%)
  between operations  2.57 us (2%)
    ppermute x8, starting transfers between devices, with_halo(): before = lax.ppermute(last, axis, up)  31.2 us
    unnamed x9, local copies, waits for them, and re-layouts  20.5 us
    ppermute x8, starting transfers between devices, with_halo(): after = lax.ppermute(leading, axis, down)  10.5 us
    all_to_all x1, waiting for transfers between devices, on_device(): lax.all_to_all(leaving, 'mem', split_axis=4, concat_axis=4, tiled=True)  8.63 us
    all_to_all x1, waiting for transfers between devices, on_device(): lax.all_to_all(outgoing(phi_owned, first_tile, columns), 'mem', split_axi...  8.36 us
    all_to_all x1, starting transfers between devices, on_device(): lax.all_to_all(leaving, 'mem', split_axis=4, concat_axis=4, tiled=True)  7.57 us
    all_to_all x1, starting transfers between devices, on_device(): lax.all_to_all(outgoing(phi_owned, first_tile, columns), 'mem', split_axi...  7.41 us
    ppermute x8, waiting for transfers between devices, with_halo(): after = lax.ppermute(leading, axis, down)  6.82 us
  transfers between devices with their start and end apart: 18, of which 7 were waited for; matrix products, arithmetic and copies ran while one was open for 4% of the time, Pallas kernels for 0%

commit v1 on v0

v1 whole, which is shorter than its diff:
```python
import functools

import jax
import jax.numpy as jnp
from jax import lax
from jax.experimental import pallas as pl
from jax.experimental.pallas import tpu as pltpu
from jax.sharding import PartitionSpec as P

STEPS = 4
TIME_STEP = 0.5
EPSILON = 1e-06
LANES = 128
F32 = jnp.float32


def roll(x, shift, axis):
    shift = shift % x.shape[axis]
    return x if shift == 0 else pltpu.roll(x, shift, axis)


def dot(a, b, dims):
    return lax.dot_general(
        a, b, (dims, ((), ())), precision=lax.Precision.HIGHEST, preferred_element_type=F32
    )


def kernel(
    columns, groups, phi_ref, place_ref, live_ref, arrive_ref, depart_ref, links_ref, out_ref,
    leave, land, back, home, up, down, from_below, from_above, right, left, from_left, from_right,
    level, sign, out_send, out_recv, back_send, back_recv, side_send, side_recv,
):
    edge = phi_ref.shape[0]
    rows = arrive_ref.shape[0]
    halo = STEPS
    wide = 2 * edge
    layers = edge + 2 * halo
    me, grp = lax.axis_index("mem"), lax.axis_index("grp")
    has_left, has_right = me > 0, me < columns - 1
    has_below, has_above = grp > 0, grp < groups - 1

    for ref in (from_below, from_above, from_left, from_right):
        ref[...] = jnp.zeros_like(ref)

    barrier = pltpu.get_barrier_semaphore()
    for d in range(1, columns):
        pl.semaphore_signal(barrier, inc=1, device_id={"mem": lax.rem(me + d, columns)},
                            device_id_type=pl.DeviceIdType.MESH)

    @pl.when(has_below)
    def _():
        pl.semaphore_signal(barrier, inc=1, device_id={"grp": grp - 1},
                            device_id_type=pl.DeviceIdType.MESH)

    @pl.when(has_above)
    def _():
        pl.semaphore_signal(barrier, inc=1, device_id={"grp": grp + 1},
                            device_id_type=pl.DeviceIdType.MESH)

    def exchange(source, target, send, recv):
        started = []
        for d in range(1, columns):
            peer = lax.rem(me + d, columns)
            copy = pltpu.make_async_remote_copy(
                src_ref=source.at[peer], dst_ref=target.at[me],
                send_sem=send.at[d], recv_sem=recv.at[d],
                device_id={"mem": peer}, device_id_type=pl.DeviceIdType.MESH)
            copy.start()
            started.append(copy)
        target[me] = source[me]
        for d in range(1, columns):
            origin = lax.rem(me + columns - d, columns)
            pltpu.make_async_remote_copy(
                src_ref=source.at[origin], dst_ref=target.at[origin],
                send_sem=send.at[d], recv_sem=recv.at[d],
                device_id={"mem": origin}, device_id_type=pl.DeviceIdType.MESH).wait_recv()
        return started

    def shift_copy(source, target, index, axis, peer):
        return pltpu.make_async_remote_copy(
            src_ref=source, dst_ref=target, send_sem=side_send.at[index],
            recv_sem=side_recv.at[index], device_id={axis: peer},
            device_id_type=pl.DeviceIdType.MESH)

    def both_ways(axis, here, more, less, ahead, behind, target_of_ahead, target_of_behind, base):
        to_ahead = shift_copy(ahead, target_of_ahead, base, axis, here + 1)
        to_behind = shift_copy(behind, target_of_behind, base + 1, axis, here - 1)
        pl.when(more)(to_ahead.start)
        pl.when(less)(to_behind.start)
        pl.when(less)(to_ahead.wait_recv)
        pl.when(more)(to_behind.wait_recv)
        pl.when(more)(to_ahead.wait_send)
        pl.when(less)(to_behind.wait_send)

    cells = jnp.concatenate(
        [phi_ref[2 * pair + k, y] for pair in range(edge // 2) for y in range(edge) for k in range(2)],
        axis=0)
    leave[...] = dot(place_ref[...], cells, ((1,), (1,))).reshape(leave.shape)

    tiles = links_ref.shape[1]
    chosen = (lax.broadcasted_iota(jnp.int32, (rows, tiles), 0) * columns + me
              == lax.broadcasted_iota(jnp.int32, (rows, tiles), 1))

    def link(face):
        there = jnp.where(links_ref[face:face + 1, :] >= 0, 1.0, 0.0).astype(F32)
        value = jnp.sum(jnp.where(chosen, there, 0.0), axis=1, keepdims=True)
        return jnp.broadcast_to(value, (rows, LANES))

    link_x = [link(0), link(1)]
    link_y = link(2)
    link_z = [link(4), link(5)]
    lane = lax.broadcasted_iota(jnp.int32, (rows, LANES), 1)
    z = lane % wide

    pl.semaphore_wait(barrier, columns - 1 + has_below.astype(jnp.int32) + has_above.astype(jnp.int32))
    sent = exchange(leave, land, out_send, out_recv)

    packed = dot(arrive_ref[...], land[...].reshape(-1, land.shape[2]), ((1,), (0,)))
    mine = []
    for pair in range(edge // 2):
        both = packed[:, pair * LANES:(pair + 1) * LANES]
        mine += [roll(both, halo, 1), roll(both, halo - edge, 1)]

    parts = mine + [link_y] + link_x
    slots = up.shape[0]
    for q in range(slots):
        high, low = jnp.zeros((rows, LANES), F32), jnp.zeros((rows, LANES), F32)
        for k in range(4):
            if 4 * q + k < len(parts):
                inside = (z >= halo * k) & (z < halo * (k + 1))
                part = parts[4 * q + k]
                high = jnp.where(inside, roll(part, halo * k - edge, 1), high)
                low = jnp.where(inside, roll(part, halo * k - halo, 1), low)
        up[q] = high
        down[q] = low
    both_ways("grp", grp, has_above, has_below, up, down, from_below, from_above, 0)

    filled = []
    for i, part in enumerate(parts):
        q, k = divmod(i, 4)
        below = roll(from_below[q], -halo * k, 1)
        above = roll(from_above[q], halo + edge - halo * k, 1)
        filled.append(jnp.where(z < halo, below, jnp.where(z >= halo + edge, above, part)))
    mine, link_y, link_x = filled[:edge], filled[edge], filled[edge + 1:]
    link_z = jnp.where(z == halo, link_z[0], jnp.where(z == halo + edge, link_z[1],
                       jnp.where(z == 0, 0.0, 1.0)))
    link_y = jnp.where(lane < wide, link_y, 1.0)

    for k in range(halo):
        right[k] = mine[edge - halo + k]
        left[k] = mine[k]
    for ref in (right, left):
        ref[halo] = link_y
        ref[halo + 1] = link_z
    both_ways("mem", me, has_right, has_left, right, left, from_left, from_right, 2)

    masks_y = [from_left[halo], link_y, from_right[halo]]
    masks_z = [from_left[halo + 1], link_z, from_right[halo + 1]]
    for i in range(layers):
        if i < halo:
            value = from_left[i]
        elif i < halo + edge:
            value = mine[i - halo]
        else:
            value = from_right[i - halo - edge]
        level[0, i] = value
        sign[i] = value / jnp.sqrt(value * value + 1.0)

    for step in range(STEPS):
        now, later = step % 2, (step + 1) % 2
        gap = None
        for i in range(step + 1, layers - 1 - step):
            region = 0 if i < halo else (1 if i < halo + edge else 2)
            mask_y, mask_z = masks_y[region], masks_z[region]
            value, field = level[now, i], sign[i]
            side = jnp.where(field > 0, 1.0, -1.0)

            def across(j):
                change = level[now, j] - level[now, j - 1]
                if j == halo:
                    change = change * link_x[0]
                elif j == halo + edge:
                    change = change * link_x[1]
                return change

            gap = across(i) if gap is None else gap
            ahead = across(i + 1)
            most = jnp.maximum(jnp.maximum(side * gap, -(side * ahead)), 0.0)
            squares = most * most
            gap = ahead

            turned = roll(value, wide, 1)
            before = jnp.where(lane < wide, roll(turned, 1, 0), turned)
            behind = (value - before) * mask_y
            turned = roll(behind, -wide, 1)
            ahead = jnp.where(lane >= LANES - wide, roll(turned, -1, 0), turned)
            most = jnp.maximum(jnp.maximum(side * behind, -(side * ahead)), 0.0)
            squares = squares + most * most

            behind = (value - roll(value, 1, 1)) * mask_z
            ahead = roll(behind, -1, 1)
            most = jnp.maximum(jnp.maximum(side * behind, -(side * ahead)), 0.0)
            squares = squares + most * most
            level[later, i] = value - TIME_STEP * field * (jnp.sqrt(squares + EPSILON) - 1.0)

    last = STEPS % 2
    pairs = []
    for pair in range(edge // 2):
        first, second = level[last, halo + 2 * pair], level[last, halo + 2 * pair + 1]
        pairs.append(jnp.where(z < edge, roll(first, -halo, 1), roll(second, edge - halo, 1)))
    final = jnp.concatenate(pairs, axis=1)
    back[...] = dot(depart_ref[...], final, ((1,), (0,))).reshape(back.shape)
    sent += exchange(back, home, back_send, back_recv)

    owned = dot(live_ref[...], home[...].reshape(-1, home.shape[2]), ((1,), (0,))).T
    for pair in range(edge // 2):
        for y in range(edge):
            for k in range(2):
                at = ((pair * edge + y) * 2 + k) * edge
                out_ref[2 * pair + k, y] = owned[at:at + edge]
    for copy in sent:
        copy.wait_send()


def on_device(phi_owned, band_counts, neighbours):
    edge, own_slots = phi_owned.shape[0], phi_owned.shape[3]
    columns, groups = lax.axis_size("mem"), lax.axis_size("grp")
    me = lax.axis_index("mem")
    rows = neighbours.shape[2] // columns
    depth = -(-own_slots // columns)
    padded = -(-depth // 8) * 8
    counts = band_counts[0]
    owners = jnp.arange(columns, dtype=jnp.int32)
    first = jnp.sum(jnp.where(owners < me, counts, 0))
    count = jnp.sum(jnp.where(owners == me, counts, 0))
    slot = jnp.arange(own_slots, dtype=jnp.int32)[None, :]
    entry = jnp.arange(columns * padded, dtype=jnp.int32)
    block, place = entry // padded, entry % padded
    chosen = ((first + slot) % columns == block[:, None]) & (slot // columns == place[:, None])
    placing = chosen.astype(F32)
    living = (chosen & (slot < count)).astype(F32).T
    starts = jnp.sum(jnp.where(owners[:, None] < block[None, :], counts[:, None], 0), axis=0)
    lengths = jnp.sum(jnp.where(owners[:, None] == block[None, :], counts[:, None], 0), axis=0)
    offset = (jnp.arange(rows, dtype=jnp.int32) * columns + me)[:, None] - starts[None, :]
    arrive = ((offset >= 0) & (offset < lengths[None, :])
              & (jnp.maximum(offset, 0) // columns == place[None, :])).astype(F32)
    halo, cells = STEPS, edge * edge * edge
    vmem = pl.BlockSpec(memory_space=pltpu.VMEM)
    buffer = pltpu.VMEM((columns, padded, cells), F32)
    strip = pltpu.VMEM((-(-(edge + 3) // 4), rows, LANES), F32)
    face = pltpu.VMEM((halo + 2, rows, LANES), F32)
    layers = edge + 2 * halo
    return pl.pallas_call(
        functools.partial(kernel, columns, groups),
        out_shape=jax.ShapeDtypeStruct(phi_owned.shape, F32),
        in_specs=[vmem] * 6,
        out_specs=vmem,
        scratch_shapes=[buffer] * 4 + [strip] * 4 + [face] * 4 + [
            pltpu.VMEM((2, layers, rows, LANES), F32),
            pltpu.VMEM((layers, rows, LANES), F32),
        ] + [pltpu.SemaphoreType.DMA((columns,))] * 4 + [pltpu.SemaphoreType.DMA((4,))] * 2,
        compiler_params=pltpu.CompilerParams(collective_id=0, has_side_effects=True),
    )(phi_owned, placing, living, arrive, arrive.T, neighbours[0])


def solution(mesh):
    return jax.shard_map(
        on_device,
        mesh=mesh,
        in_specs=(P(None, None, None, ("grp", "mem")), P("grp", None), P("grp", None, None)),
        out_specs=P(None, None, None, ("grp", "mem")),
        check_vma=False,
    )
```

time: 151 us -> 38.1 us (0.25)
  the two profiles are of different devices: /device:TPU:0 before, /device:TPU:13 now
where the time goes in v1:
time: 38.1 us; the launch traced here: 37.9 us
  Pallas kernels  30.6 us (80%)
  other arithmetic  4.36 us (11%)
  local copies, waits for them, and re-layouts  2.94 us (8%)
    pallas_call x1, Pallas kernels, on_device(): pl.pallas_call(functools.partial(kernel, columns, groups), out_shape=jax....  30.6 us
    unnamed x6, local copies, waits for them, and re-layouts  2.94 us
    convert_element_type x2, other arithmetic, on_device(): arrive = ((offset >= 0) & (offset < lengths[None, :]) & (jnp.maximum(offs...  1.43 us
    convert_element_type x1, other arithmetic, on_device(): living = (chosen & (slot < count)).astype(F32).T  0.78 us

profile of v1, /device:TPU:13, one launch (start us, length us, event | category | flops | bytes accessed | tf_op | source)
XLA Modules:
  0.0 37.9 jit_solution(15485947012287026779)
XLA Ops:
  0.0 0.0 copy-start.1
  0.0 0.6 %copy-done.1 = s32[1,16]{1,0:T(1,128)S(1)} copy-done((s32[1,16]{1,0:T(1,128)S(1)}, s32[1,16]{1,0:T(1,128)}, u32[]{:S(2)}) %copy-start.1) | copy-done | bytes 88
  0.7 0.7 %fusion.21 = (s32[]{:T(128)}, s32[]{:T(128)}) fusion(s32[]{:T(128)S(6)} %axis_index.12, s32[1,16]{1,0:T(1,128)S(1)} %copy-done.1), kind=kLoop, calls=%fused_computation.49 | loop fusion | flops 94 | bytes 76 | tf_op jit(solution)/shard_map/reduce_sum | solution.py:235
  1.4 0.6 %iota_compare_fusion.2 = pred[128]{0:T(512)(128)(4,1)S(1)} fusion(s32[]{:T(128)} %get-tuple-element.7), kind=kLoop, calls=%fused_computation.52 | loop fusion | flops 128 | bytes 132 | tf_op jit(solution)/shard_map/lt | solution.py:241
  2.0 0.7 %and_select_fusion.2 = (s32[128]{0:T(128)S(1)}, s32[128]{0:T(128)S(1)}) fusion(s32[]{:T(128)} %get-tuple-element.8), kind=kLoop, calls=%fused_computation.40 | loop fusion | flops 2560 | bytes 1028 | tf_op jit(solution)/shard_map/jit(floor_divide)/jit(_where)/select_n | solution.py:238
  2.7 0.1 select_reduce_fusion.1
  2.8 0.0 copy-start
  2.8 0.7 %fusion.18.arrive_ref = f32[32,128]{1,0:T(8,128)} fusion(s32[128]{0:T(128)S(1)} %get-tuple-element.11, s32[128]{0:T(128)S(1)} %get-tuple-element.6, s32[128]{0:T(128)S(1)} %get-tuple-element.5, s32[32]{0:T(128)S(1)} %multiply_add_fusion), kind=kLoop, calls=%fused_computation.29 | loop fusion | flops 65536 | bytes 18048 | tf_op jit(solution)/shard_map/convert_element_type | solution.py:246
  3.5 0.0 copy-done
  3.5 0.6 %copy.7 = s32[1,6,512]{2,1,0:T(8,128)} copy(s32[1,6,512]{2,0,1:T(1,128)S(1)} %copy-done) | data formatting | bytes 24576
  4.1 0.7 %fusion.8.depart_ref = f32[128,32]{1,0:T(8,128)} fusion(s32[32]{0:T(128)S(1)} %multiply_add_fusion, s32[128]{0:T(128)S(1)} %get-tuple-element.11, s32[128]{0:T(128)S(1)} %get-tuple-element.6, s32[128]{0:T(128)S(1)} %get-tuple-element.5), kind=kLoop, calls=%fused_computation.12 | loop fusion | flops 65536 | bytes 18048 | tf_op jit(solution)/shard_map/convert_element_type | solution.py:246
  4.9 0.8 %and_convert_fusion = (f32[128,128]{1,0:T(8,128)}, f32[128,128]{1,0:T(8,128)}) fusion(s32[128]{0:T(128)S(1)} %get-tuple-element.11, s32[128]{0:T(128)S(1)} %get-tuple-element.13, s32[128]{0:T(128)S(1)} %get-tuple-element.12, s32[128]{0:T(128)S(1)} %get-tuple-element.14, pred[128]{0:T(512)(128)(4,1)S(1)} %iota_compare_fusion.2), kind=kLoop, calls=%fused_computation.14 | loop fusion | flops 147456 | bytes 133248 | tf_op jit(solution)/shard_map/convert_element_type | solution.py:241
  5.6 30.6 %shard_map.37 = f32[8,8,8,128]{3,2,1,0:T(8,128)} custom-call(f32[8,8,8,128]{3,2,1,0:T(8,128)} %phi_ref.1, f32[128,128]{1,0:T(8,128)} %get-tuple-element.10.place_ref, f32[128,128]{1,0:T(8,128)} %get-tuple-element.9.live_ref, f32[32,128]{1,0:T(8,128)} %fusion.18.arrive_ref, f32[128,32]{1,0:T(8,128)} %fusion.8.depart_ref, s32[6,512]{1,0:T(8,128)} %bitcast.6), custom_call_target="tpu_custom_call" | custom-call | tf_op jit(solution)/shard_map/pallas_call | solution.py:253
  36.2 1.7 %copy.9 = f32[8,8,8,128]{3,2,1,0:T(8,128)} copy(f32[8,8,8,128]{3,2,1,0:T(8,128)} %shard_map.37) | data formatting | bytes 524288
  (2 shorter events, 0.0 us)
Async XLA Ops:
  0.0 0.7 %copy-start.1 = (s32[1,16]{1,0:T(1,128)S(1)}, s32[1,16]{1,0:T(1,128)}, u32[]{:S(2)}) copy-start(s32[1,16]{1,0:T(1,128)} %param.4) | copy-start | bytes 196
  2.8 0.7 %copy-start = (s32[1,6,512]{2,0,1:T(1,128)S(1)}, s32[1,6,512]{2,0,1:T(1,128)}, u32[]{:S(2)}) copy-start(s32[1,6,512]{2,0,1:T(1,128)} %param.5) | copy-start | bytes 36868

commit v2 on v1

--- a/solution.py
+++ b/solution.py
@@ -26,12 +26,14 @@
 
 
 def kernel(
-    columns, groups, phi_ref, place_ref, live_ref, arrive_ref, depart_ref, links_ref, out_ref,
+    columns, groups, phi_ref, counts_ref, links_ref, out_ref,
     leave, land, back, home, up, down, from_below, from_above, right, left, from_left, from_right,
     level, sign, out_send, out_recv, back_send, back_recv, side_send, side_recv,
 ):
     edge = phi_ref.shape[0]
-    rows = arrive_ref.shape[0]
+    own_slots = phi_ref.shape[3]
+    padded, tiles = leave.shape[1], links_ref.shape[2]
+    rows = tiles // columns
     halo = STEPS
     wide = 2 * edge
     layers = edge + 2 * halo
@@ -92,18 +94,38 @@
         pl.when(more)(to_ahead.wait_send)
         pl.when(less)(to_behind.wait_send)
 
+    count_of = [counts_ref[0, m] for m in range(columns)]
+    first, count = jnp.int32(0), jnp.int32(0)
+    for m in range(columns):
+        first = first + jnp.where(m < me, count_of[m], 0)
+        count = count + jnp.where(m == me, count_of[m], 0)
+    entries = columns * padded
+    slot = lax.broadcasted_iota(jnp.int32, (1, own_slots), 1)
+    key = (first + slot) % columns * padded + slot // columns
+    chosen = lax.broadcasted_iota(jnp.int32, (entries, own_slots), 0) == key
+    placing = jnp.where(chosen, 1.0, 0.0).astype(F32)
+    entry = lax.broadcasted_iota(jnp.int32, (1, entries), 1)
+    block, place = entry // padded, entry % padded
+    start, length = jnp.zeros((1, entries), jnp.int32), jnp.zeros((1, entries), jnp.int32)
+    for m in range(columns):
+        start = start + jnp.where(block > m, count_of[m], 0)
+        length = length + jnp.where(block == m, count_of[m], 0)
+    offset = lax.broadcasted_iota(jnp.int32, (rows, entries), 0) * columns + me - start
+    begin = place * columns
+    arrive = jnp.where((offset >= begin) & (offset < begin + columns) & (offset < length),
+                       1.0, 0.0).astype(F32)
+
     cells = jnp.concatenate(
         [phi_ref[2 * pair + k, y] for pair in range(edge // 2) for y in range(edge) for k in range(2)],
         axis=0)
-    leave[...] = dot(place_ref[...], cells, ((1,), (1,))).reshape(leave.shape)
-
-    tiles = links_ref.shape[1]
-    chosen = (lax.broadcasted_iota(jnp.int32, (rows, tiles), 0) * columns + me
-              == lax.broadcasted_iota(jnp.int32, (rows, tiles), 1))
+    leave[...] = dot(placing, cells, ((1,), (1,))).reshape(leave.shape)
+
+    held = (lax.broadcasted_iota(jnp.int32, (rows, tiles), 0) * columns + me
+            == lax.broadcasted_iota(jnp.int32, (rows, tiles), 1))
 
     def link(face):
-        there = jnp.where(links_ref[face:face + 1, :] >= 0, 1.0, 0.0).astype(F32)
-        value = jnp.sum(jnp.where(chosen, there, 0.0), axis=1, keepdims=True)
+        there = jnp.where(links_ref[face] >= 0, 1.0, 0.0).astype(F32)
+        value = jnp.sum(jnp.where(held, there, 0.0), axis=1, keepdims=True)
         return jnp.broadcast_to(value, (rows, LANES))
 
     link_x = [link(0), link(1)]
@@ -115,7 +137,7 @@
     pl.semaphore_wait(barrier, columns - 1 + has_below.astype(jnp.int32) + has_above.astype(jnp.int32))
     sent = exchange(leave, land, out_send, out_recv)
 
-    packed = dot(arrive_ref[...], land[...].reshape(-1, land.shape[2]), ((1,), (0,)))
+    packed = dot(arrive, land[...].reshape(-1, land.shape[2]), ((1,), (0,)))
     mine = []
     for pair in range(edge // 2):
         both = packed[:, pair * LANES:(pair + 1) * LANES]
@@ -209,10 +231,11 @@
         first, second = level[last, halo + 2 * pair], level[last, halo + 2 * pair + 1]
         pairs.append(jnp.where(z < edge, roll(first, -halo, 1), roll(second, edge - halo, 1)))
     final = jnp.concatenate(pairs, axis=1)
-    back[...] = dot(depart_ref[...], final, ((1,), (0,))).reshape(back.shape)
+    back[...] = dot(arrive, final, ((0,), (0,))).reshape(back.shape)
     sent += exchange(back, home, back_send, back_recv)
 
-    owned = dot(live_ref[...], home[...].reshape(-1, home.shape[2]), ((1,), (0,))).T
+    living = jnp.where(slot < count, placing, 0.0)
+    owned = dot(living, home[...].reshape(-1, home.shape[2]), ((0,), (0,))).T
     for pair in range(edge // 2):
         for y in range(edge):
             for k in range(2):
@@ -225,25 +248,8 @@
 def on_device(phi_owned, band_counts, neighbours):
     edge, own_slots = phi_owned.shape[0], phi_owned.shape[3]
     columns, groups = lax.axis_size("mem"), lax.axis_size("grp")
-    me = lax.axis_index("mem")
     rows = neighbours.shape[2] // columns
-    depth = -(-own_slots // columns)
-    padded = -(-depth // 8) * 8
-    counts = band_counts[0]
-    owners = jnp.arange(columns, dtype=jnp.int32)
-    first = jnp.sum(jnp.where(owners < me, counts, 0))
-    count = jnp.sum(jnp.where(owners == me, counts, 0))
-    slot = jnp.arange(own_slots, dtype=jnp.int32)[None, :]
-    entry = jnp.arange(columns * padded, dtype=jnp.int32)
-    block, place = entry // padded, entry % padded
-    chosen = ((first + slot) % columns == block[:, None]) & (slot // columns == place[:, None])
-    placing = chosen.astype(F32)
-    living = (chosen & (slot < count)).astype(F32).T
-    starts = jnp.sum(jnp.where(owners[:, None] < block[None, :], counts[:, None], 0), axis=0)
-    lengths = jnp.sum(jnp.where(owners[:, None] == block[None, :], counts[:, None], 0), axis=0)
-    offset = (jnp.arange(rows, dtype=jnp.int32) * columns + me)[:, None] - starts[None, :]
-    arrive = ((offset >= 0) & (offset < lengths[None, :])
-              & (jnp.maximum(offset, 0) // columns == place[None, :])).astype(F32)
+    padded = -(-own_slots // (8 * columns)) * 8
     halo, cells = STEPS, edge * edge * edge
     vmem = pl.BlockSpec(memory_space=pltpu.VMEM)
     buffer = pltpu.VMEM((columns, padded, cells), F32)
@@ -253,14 +259,14 @@
     return pl.pallas_call(
         functools.partial(kernel, columns, groups),
         out_shape=jax.ShapeDtypeStruct(phi_owned.shape, F32),
-        in_specs=[vmem] * 6,
+        in_specs=[vmem, pl.BlockSpec(memory_space=pltpu.SMEM), vmem],
         out_specs=vmem,
         scratch_shapes=[buffer] * 4 + [strip] * 4 + [face] * 4 + [
             pltpu.VMEM((2, layers, rows, LANES), F32),
             pltpu.VMEM((layers, rows, LANES), F32),
         ] + [pltpu.SemaphoreType.DMA((columns,))] * 4 + [pltpu.SemaphoreType.DMA((4,))] * 2,
         compiler_params=pltpu.CompilerParams(collective_id=0, has_side_effects=True),
-    )(phi_owned, placing, living, arrive, arrive.T, neighbours[0])
+    )(phi_owned, band_counts, jnp.transpose(neighbours, (1, 0, 2)))
 
 
 def solution(mesh):

time: 38.1 us -> 32.4 us (0.85)
  other arithmetic: 4.36 us -> 0 us
  local copies, waits for them, and re-layouts: 2.94 us -> 1.67 us
    convert_element_type x3 -> x0, other arithmetic: 2.2 us -> none  [the longest x2 1.43 us: on_device(): arrive = ((offset >= 0) & (offset < lengths[None, :]) & (jnp.maximum(offs...]
    unnamed x6 -> x1, local copies, waits for them, and re-layouts: 2.94 us -> 1.67 us
    reduce_sum x2 -> x0, other arithmetic: 0.8 us -> none  [the longest x1 0.71 us: on_device(): count = jnp.sum(jnp.where(owners == me, counts, 0))]
    select_n x2 -> x0, other arithmetic: 0.7 us -> none  [on_device(): block, place = (entry // padded, entry % padded)]
    lt x1 -> x0, other arithmetic: 0.65 us -> none  [on_device(): living = (chosen & (slot < count)).astype(F32).T]
where the time goes in v2:
time: 32.4 us; the launch traced here: 32.3 us
  Pallas kernels  30.6 us (94%)
  local copies, waits for them, and re-layouts  1.67 us (5%)
    pallas_call x1, Pallas kernels, on_device(): pl.pallas_call(functools.partial(kernel, columns, groups), out_shape=jax....  30.6 us
    unnamed x1, local copies, waits for them, and re-layouts  1.67 us

profile of v2, /device:TPU:13, one launch (start us, length us, event | category | flops | bytes accessed | tf_op | source)
XLA Modules:
  0.0 32.3 jit_solution(5897279670615980489)
XLA Ops:
  0.0 30.6 %shard_map.37 = f32[8,8,8,128]{3,2,1,0:T(8,128)} custom-call(f32[8,8,8,128]{3,2,1,0:T(8,128)} %phi_ref.1, s32[1,16]{1,0:T(1,128)} %counts_ref.1, s32[6,1,512]{2,1,0:T(1,128)} %bitcast.1), custom_call_target="tpu_custom_call" | custom-call | tf_op jit(solution)/shard_map/pallas_call | solution.py:259
  30.6 1.7 %copy.5 = f32[8,8,8,128]{3,2,1,0:T(8,128)} copy(f32[8,8,8,128]{3,2,1,0:T(8,128)} %shard_map.37) | data formatting | bytes 524288

commit v3 on v2

--- a/solution.py
+++ b/solution.py
@@ -89,10 +89,15 @@
         to_behind = shift_copy(behind, target_of_behind, base + 1, axis, here - 1)
         pl.when(more)(to_ahead.start)
         pl.when(less)(to_behind.start)
-        pl.when(less)(to_ahead.wait_recv)
-        pl.when(more)(to_behind.wait_recv)
-        pl.when(more)(to_ahead.wait_send)
-        pl.when(less)(to_behind.wait_send)
+        late.extend([(more, to_ahead), (less, to_behind)])
+
+        def arrived():
+            pl.when(less)(to_ahead.wait_recv)
+            pl.when(more)(to_behind.wait_recv)
+
+        return arrived
+
+    late = []
 
     count_of = [counts_ref[0, m] for m in range(columns)]
     first, count = jnp.int32(0), jnp.int32(0)
@@ -155,7 +160,7 @@
                 low = jnp.where(inside, roll(part, halo * k - halo, 1), low)
         up[q] = high
         down[q] = low
-    both_ways("grp", grp, has_above, has_below, up, down, from_below, from_above, 0)
+    both_ways("grp", grp, has_above, has_below, up, down, from_below, from_above, 0)()
 
     filled = []
     for i, part in enumerate(parts):
@@ -174,24 +179,18 @@
     for ref in (right, left):
         ref[halo] = link_y
         ref[halo + 1] = link_z
-    both_ways("mem", me, has_right, has_left, right, left, from_left, from_right, 2)
-
-    masks_y = [from_left[halo], link_y, from_right[halo]]
-    masks_z = [from_left[halo + 1], link_z, from_right[halo + 1]]
-    for i in range(layers):
-        if i < halo:
-            value = from_left[i]
-        elif i < halo + edge:
-            value = mine[i - halo]
-        else:
-            value = from_right[i - halo - edge]
+    arrived = both_ways("mem", me, has_right, has_left, right, left, from_left, from_right, 2)
+
+    masks_y, masks_z = [None, link_y, None], [None, link_z, None]
+
+    def begin_layer(i, value):
         level[0, i] = value
         sign[i] = value / jnp.sqrt(value * value + 1.0)
 
-    for step in range(STEPS):
+    def sweep(step, low, high):
         now, later = step % 2, (step + 1) % 2
         gap = None
-        for i in range(step + 1, layers - 1 - step):
+        for i in range(low, high):
             region = 0 if i < halo else (1 if i < halo + edge else 2)
             mask_y, mask_z = masks_y[region], masks_z[region]
             value, field = level[now, i], sign[i]
@@ -224,6 +223,20 @@
             most = jnp.maximum(jnp.maximum(side * behind, -(side * ahead)), 0.0)
             squares = squares + most * most
             level[later, i] = value - TIME_STEP * field * (jnp.sqrt(squares + EPSILON) - 1.0)
+
+    for i in range(edge):
+        begin_layer(halo + i, mine[i])
+    sweep(0, halo + 1, halo + edge - 1)
+    arrived()
+    masks_y[0], masks_y[2] = from_left[halo], from_right[halo]
+    masks_z[0], masks_z[2] = from_left[halo + 1], from_right[halo + 1]
+    for i in range(halo):
+        begin_layer(i, from_left[i])
+        begin_layer(halo + edge + i, from_right[i])
+    sweep(0, 1, halo + 1)
+    sweep(0, halo + edge - 1, layers - 1)
+    for step in range(1, STEPS):
+        sweep(step, step + 1, layers - 1 - step)
 
     last = STEPS % 2
     pairs = []
@@ -243,6 +256,8 @@
                 out_ref[2 * pair + k, y] = owned[at:at + edge]
     for copy in sent:
         copy.wait_send()
+    for there, copy in late:
+        pl.when(there)(copy.wait_send)
 
 
 def on_device(phi_owned, band_counts, neighbours):

time: 32.4 us -> 32 us (0.988)
  Pallas kernels: 30.6 us -> 30.1 us
    pallas_call x1, Pallas kernels: 30.6 us -> 30.1 us  [on_device(): pl.pallas_call(functools.partial(kernel, columns, groups), out_shape=jax....]
where the time goes in v3:
time: 32 us; the launch traced here: 31.8 us
  Pallas kernels  30.1 us (94%)
  local copies, waits for them, and re-layouts  1.67 us (5%)
    pallas_call x1, Pallas kernels, on_device(): pl.pallas_call(functools.partial(kernel, columns, groups), out_shape=jax....  30.1 us
    unnamed x1, local copies, waits for them, and re-layouts  1.67 us

profile of v3, /device:TPU:13, one launch (start us, length us, event | category | flops | bytes accessed | tf_op | source)
XLA Modules:
  0.0 31.8 jit_solution(11414870456637471310)
XLA Ops:
  0.0 30.1 %shard_map.37 = f32[8,8,8,128]{3,2,1,0:T(8,128)} custom-call(f32[8,8,8,128]{3,2,1,0:T(8,128)} %phi_ref.1, s32[1,16]{1,0:T(1,128)} %counts_ref.1, s32[6,1,512]{2,1,0:T(1,128)} %bitcast.1), custom_call_target="tpu_custom_call" | custom-call | tf_op jit(solution)/shard_map/pallas_call | solution.py:274
  30.2 1.7 %copy.5 = f32[8,8,8,128]{3,2,1,0:T(8,128)} copy(f32[8,8,8,128]{3,2,1,0:T(8,128)} %shard_map.37) | data formatting | bytes 524288
